TPU v7x, 32 devices: a whole 2x2x4 slice. The times are simulated.
32 devices in a mesh: groups: 2 (over y), expert: 4 (over z), tensor: 2 (over x), sub: 2 (over core).
Axes of the slice: x: 2, y: 2, z: 4, core: 2. Of those that a mesh axis runs over, the one named last changes fastest.
Arguments:
- tokens: bfloat16 [48, 7168], P(('groups', 'expert', 'tensor'), 'sub'), parts along dimension 0, may hold values from -6 to 6
- expert_ids: int32 [48, 8], P(('groups', 'expert', 'tensor')), parts along dimension 0, may hold values from 0 to 15, all different within a row; in each aligned block of 3 rows (0 to 2, 3 to 5, ...) at most 2 rows name the same one
- gate_weights: float32 [48, 8], P(('groups', 'expert', 'tensor')), parts along dimension 0, may hold values from 0.1 to 0.6
- gate_proj: bfloat16 [16, 1024, 7168], P('expert', 'tensor', 'sub'), may hold values from -0.0625 to 0.0625
- up_proj: bfloat16 [16, 1024, 7168], P('expert', 'tensor', 'sub'), may hold values from -0.0625 to 0.0625
- down_proj: bfloat16 [16, 1024, 7168], P('expert', 'tensor', 'sub'), may hold values from -0.1875 to 0.1875
Outputs:
- blended: bfloat16 [48, 7168], P(('groups', 'expert', 'tensor'), 'sub'), parts along dimension 0
There are 2 independent parts, one for each index of `groups`. A program takes and returns all parts, laid end to end along the dimension named above; an argument that names none is the same for every part. Nothing has to cross between parts.
Inputs may be any that keep to these rules, and one draw needn't show every extreme that they name: `expert_ids`: each row names 8 different experts. Among the rows of one owner (aligned blocks of 3 rows) no expert is named by more than 2 rows, a bound that some block reaches.
All inputs are finite; a program needn't handle non-finite values.
Results may differ from a plain program's by a relative error of at most 0.02.
Values may be sent and summed in bfloat16 or wider, within the bound.
A program may use at most 128 MiB of HBM per device.

v0:
```python
import jax
import jax.numpy as jnp
from jax import lax
from jax.sharding import PartitionSpec as P

SLOTS = 2


def per_device(tokens, expert_ids, gate_weights, gate_proj, up_proj, down_proj):
    expert_count = lax.axis_size("expert")
    tensor_count = lax.axis_size("tensor")
    local_count = gate_proj.shape[0]
    total_experts = expert_count * local_count
    features = tokens.shape[1]
    owned = tokens.shape[0]
    labels = jnp.arange(total_experts, dtype=jnp.int32)
    chosen = expert_ids[:, :, None] == labels[None, None, :]
    picked = jnp.sum(chosen.astype(jnp.int32), axis=1)
    before = jnp.cumsum(picked, axis=0) - picked
    slot_ids = jnp.arange(SLOTS, dtype=jnp.int32)
    placed = (picked[:, :, None] == 1) & (before[:, :, None] == slot_ids[None, None, :])
    placed_flat = placed.reshape(owned, total_experts * SLOTS)
    outgoing = jnp.dot(
        placed_flat.astype(jnp.bfloat16).T, tokens, preferred_element_type=jnp.float32
    ).astype(jnp.bfloat16)
    slab = local_count * SLOTS * features
    outgoing = outgoing.reshape(expert_count, slab)
    peers = expert_count * tensor_count
    copies = jnp.broadcast_to(outgoing[:, None, :], (expert_count, tensor_count, slab)).reshape(
        peers, slab
    )
    arrived = lax.all_to_all(copies, ("expert", "tensor"), split_axis=0, concat_axis=0, tiled=True)
    rows_in = jnp.moveaxis(arrived.reshape(peers, local_count, SLOTS, features), 1, 0)
    rows_in = rows_in.reshape(local_count, peers * SLOTS, features)
    gate_part = jnp.einsum("lrd,lfd->lrf", rows_in, gate_proj, preferred_element_type=jnp.float32)
    up_part = jnp.einsum("lrd,lfd->lrf", rows_in, up_proj, preferred_element_type=jnp.float32)
    gate_full, up_full = (
        lax.psum(gate_part.astype(jnp.bfloat16), "sub").astype(jnp.float32),
        lax.psum(up_part.astype(jnp.bfloat16), "sub").astype(jnp.float32),
    )
    hidden = (jax.nn.silu(gate_full) * up_full).astype(jnp.bfloat16)
    partial_value = jnp.einsum(
        "lrf,lfd->lrd", hidden, down_proj, preferred_element_type=jnp.float32
    ).astype(jnp.bfloat16)
    partial_value = jnp.moveaxis(
        partial_value.reshape(local_count, peers, SLOTS, features), 0, 1
    ).reshape(peers, slab)
    returned = lax.all_to_all(
        partial_value, ("expert", "tensor"), split_axis=0, concat_axis=0, tiled=True
    )
    returned = returned.reshape(expert_count, tensor_count, slab)
    results = jnp.sum(returned.astype(jnp.float32), axis=1).reshape(total_experts * SLOTS, features)
    weight_table = jnp.sum(gate_weights[:, :, None] * chosen.astype(jnp.float32), axis=1)
    mixing = (weight_table[:, :, None] * placed.astype(jnp.float32)).reshape(
        owned, total_experts * SLOTS
    )
    blended = jnp.dot(mixing, results, precision=lax.Precision.HIGHEST)
    return blended.astype(jnp.bfloat16)


def solution(mesh):
    placed = (
        P(("groups", "expert", "tensor"), "sub"),
        P(("groups", "expert", "tensor"), None),
        P(("groups", "expert", "tensor"), None),
        P("expert", "tensor", "sub"),
        P("expert", "tensor", "sub"),
        P("expert", "tensor", "sub"),
    )
    return jax.shard_map(
        per_device,
        mesh=mesh,
        in_specs=placed,
        out_specs=P(("groups", "expert", "tensor"), "sub"),
        check_vma=False,
    )
```

profile of v0, /device:TPU:0, one launch (start us, length us, event | category | flops | bytes accessed | tf_op | source)
XLA Modules:
  0.0 119.9 jit_solution(9019192052215831962)
XLA Ops:
  6.5 0.0 copy-start
  6.5 0.0 all-reduce.3.cloned.1.call-start
  6.5 0.8 convert_reduce_fusion.1
  7.4 0.1 and.21
  7.4 0.1 and.23
  7.6 0.1 eq.66
  7.6 0.1 eq.61
  7.7 0.1 eq.64
  7.8 0.0 copy-done
  7.8 0.3 convolution_convert_fusion.1
  8.1 0.2 broadcast_in_dim.4
  8.3 0.2 broadcast_in_dim.5
  8.5 0.5 all_to_all.16
  9.0 0.5 broadcast.69
  9.5 3.5 %reduce.3 = bf16[8,28672]{1,0:T(8,128)(2,1)S(1)} reduce(bf16[8,1,28672]{2,1,0:T(2,128)(2,1)S(1)} %all_to_all.16, bf16[]{:T(256)} %broadcast.69), dimensions={1}, to_apply=%all_to_all.16.reduce_sub_computation | reduce | bytes 917506 | tf_op jit(solution)/shard_map/all_to_all | solution.py:32
  13.0 0.3 reshape.94
  13.4 20.3 %all_to_all.20 = bf16[8,2,14336]{2,1,0:T(2,128)(2,1)S(1)} all-to-all(bf16[8,2,14336]{2,1,0:T(2,128)(2,1)S(1)} %reshape.94), channel_id=1, replica_groups=mesh['groups'=2,'expert'=4,'tensor'=2,'sub'=2] {'expert','tensor'}, dimensions={0} | all-to-all | bytes 917504 | tf_op jit(solution)/shard_map/all_to_all | solution.py:32
  33.7 0.5 reshape.95
  34.1 2.9 %reduce = bf16[8,28672]{1,0:T(8,128)(2,1)S(1)} reduce(bf16[8,1,28672]{2,1,0:T(2,128)(2,1)S(1)} %reshape.95, bf16[]{:T(256)} %constant.17), dimensions={1}, to_apply=%all_to_all.13.reduce_sub_computation | reduce | bytes 917506 | tf_op jit(solution)/shard_map/all_to_all | solution.py:32
  37.0 0.3 reshape.87
  37.3 0.3 copy.17
  37.7 0.2 reshape.88
  37.9 9.7 %convolution_convert_fusion.3 = bf16[4,16,512]{2,1,0:T(8,128)(2,1)} fusion(bf16[4,16,3584]{2,1,0:T(8,128)(2,1)S(1)} %reshape.88, bf16[4,512,3584]{2,1,0:T(8,128)(2,1)} %param.10), kind=kOutput, calls=%fused_computation.3 | convolution fusion | flops 234913792 | bytes 15204352 | tf_op jit(solution)/shard_map/lrd,lfd->lrf/dot_general | solution.py:36
  47.5 9.7 %convolution_convert_fusion.4 = bf16[4,16,512]{2,1,0:T(8,128)(2,1)} fusion(bf16[4,16,3584]{2,1,0:T(8,128)(2,1)S(1)} %reshape.88, bf16[4,512,3584]{2,1,0:T(8,128)(2,1)} %param.9), kind=kOutput, calls=%fused_computation.4 | convolution fusion | flops 234913792 | bytes 15204352 | tf_op jit(solution)/shard_map/lrd,lfd->lrf/dot_general | solution.py:35
  57.2 0.0 copy-start.1
  57.2 0.0 copy-start.2
  57.2 0.0 all-reduce.3.cloned.1.call-update
  57.3 17.1 %all-reduce.3.cloned.1.call-done = (bf16[4,16,512]{2,1,0:T(8,128)(2,1)}, bf16[4,16,512]{2,1,0:T(8,128)(2,1)}) async-done(((bf16[4,16,512]{2,1,0:T(8,128)(2,1)}, bf16[4,16,512]{2,1,0:T(8,128)(2,1)}), (bf16[4,16,512]{2,1,0:T(8,128)(2,1)}, bf16[4,16,512]{2,1,0:T(8,128)(2,1)})) %all-reduce.3.cloned.1.call-update) | async-done | bytes 131088 | tf_op jit(solution)/shard_map/psum | solution.py:39
  74.4 7.3 %convolution_convert_fusion = bf16[4,16,3584]{2,1,0:T(8,128)(2,1)S(1)} fusion(bf16[4,512,3584]{2,1,0:T(8,128)(2,1)} %param.11, bf16[4,16,512]{2,1,0:T(8,128)(2,1)} %get-tuple-element.5, bf16[4,16,512]{2,1,0:T(8,128)(2,1)} %get-tuple-element.6), kind=kOutput, calls=%fused_computation | convolution fusion | flops 235372544 | bytes 15269888 | tf_op jit(solution)/shard_map/lrf,lfd->lrd/dot_general | solution.py:42
  81.6 0.2 reshape.89
  81.8 0.3 copy.22
  82.1 0.6 all_to_all.17
  82.8 3.5 %reduce.4 = bf16[8,28672]{1,0:T(8,128)(2,1)S(1)} reduce(bf16[8,1,28672]{2,1,0:T(2,128)(2,1)S(1)} %all_to_all.17, bf16[]{:T(256)} %broadcast.69), dimensions={1}, to_apply=%all_to_all.17.reduce_sub_computation | reduce | bytes 917506 | tf_op jit(solution)/shard_map/all_to_all | solution.py:48
  86.3 1.1 reshape.96
  87.4 5.8 %all-to-all-start.1 = ((bf16[8,2,14336]{2,1,0:T(2,128)(2,1)}), bf16[8,2,14336]{2,1,0:T(2,128)(2,1)S(1)}, u32[]{:S(2)}, u32[]{:S(2)}) async-start(bf16[8,2,14336]{2,1,0:T(2,128)(2,1)} %reshape.96), calls=%async_computation.1 | async-start | bytes 917504 | tf_op jit(solution)/shard_map/all_to_all | solution.py:48
  93.2 0.0 copy-done.1
  93.2 0.0 copy-done.2
  93.2 0.1 select_reduce_fusion
  93.3 0.1 fusion.8
  93.4 0.1 mul.29
  93.5 13.2 %all-to-all-done.1 = bf16[8,2,14336]{2,1,0:T(2,128)(2,1)S(1)} async-done(((bf16[8,2,14336]{2,1,0:T(2,128)(2,1)}), bf16[8,2,14336]{2,1,0:T(2,128)(2,1)S(1)}, u32[]{:S(2)}, u32[]{:S(2)}) %all-to-all-start.1) | async-done | bytes 458784 | tf_op jit(solution)/shard_map/all_to_all | solution.py:48
  106.7 0.5 reshape.97
  107.2 2.7 %convert_reduce_fusion = f32[8,28672]{1,0:T(8,128)S(1)} fusion(bf16[8,1,28672]{2,1,0:T(2,128)(2,1)S(1)} %reshape.97), kind=kLoop, calls=%fused_computation.5 | loop fusion | flops 229376 | bytes 1376256 | tf_op jit(solution)/shard_map/convert_element_type | solution.py:52
  109.9 0.5 reshape.91
  110.4 1.3 %reduce_sum.29 = f32[4,28672]{1,0:T(4,128)S(1)} reduce(f32[4,2,28672]{2,1,0:T(2,128)S(1)} %reshape.91, f32[]{:T(128)} %constant.12.clone.1), dimensions={1}, to_apply=%region_5.6 | reduce | flops 114688 | bytes 1376260 | tf_op jit(solution)/shard_map/reduce_sum | solution.py:52
  111.7 0.3 reshape.90
  112.1 0.9 convolution_convert_fusion.2
  (4 shorter events, 0.1 us)
Async XLA Ops:
  6.5 1.3 %copy-start = (bf16[3,3584]{1,0:T(4,128)(2,1)S(1)}, bf16[3,3584]{1,0:T(4,128)(2,1)}, u32[]{:S(2)}) copy-start(bf16[3,3584]{1,0:T(4,128)(2,1)} %param.6) | copy-start | bytes 64516
  6.5 67.8 %all-reduce.3.cloned.1.call-start = ((), (), s32[]{:S(2)}) async-start(), calls=%async_computation.2 | async-start | bytes 262144 | tf_op jit(solution)/shard_map/psum | solution.py:39
  57.2 36.0 %copy-start.1 = (s32[3,8]{1,0:T(4,128)S(1)}, s32[3,8]{1,0:T(4,128)}, u32[]{:S(2)}) copy-start(s32[3,8]{1,0:T(4,128)} %param.7) | copy-start | bytes 292
  57.2 36.0 %copy-start.2 = (f32[3,8]{1,0:T(4,128)S(1)}, f32[3,8]{1,0:T(4,128)}, u32[]{:S(2)}) copy-start(f32[3,8]{1,0:T(4,128)} %param.8) | copy-start | bytes 292
  87.4 19.3 %all-to-all-start.1 = ((bf16[8,2,14336]{2,1,0:T(2,128)(2,1)}), bf16[8,2,14336]{2,1,0:T(2,128)(2,1)S(1)}, u32[]{:S(2)}, u32[]{:S(2)}) async-start(bf16[8,2,14336]{2,1,0:T(2,128)(2,1)} %reshape.96), calls=%async_computation.1 | async-start | bytes 917504 | tf_op jit(solution)/shard_map/all_to_all | solution.py:48
Sparse Core Ops, SparseCore 0:
  57.4 16.9 all-reduce.2
where the time goes:
time: 120 us
  waiting for transfers between devices  30.3 us (25%)
  matrix products  27.8 us (23%)
  blocking collectives  20.3 us (17%)
  other arithmetic  15 us (12%)
  between operations  13.6 us (11%)
  local copies, waits for them, and re-layouts  7.07 us (6%)
  starting transfers between devices  5.82 us (5%)
    all_to_all x1, blocking collectives, per_device(): lax.all_to_all(copies, ('expert', 'tensor'), split_axis=0, concat_axis=0,...  20.3 us
    psum x1, waiting for transfers between devices, per_device(): lax.psum(up_part.astype(jnp.bfloat16), 'sub').astype(jnp.float32)  17.1 us
    all_to_all x1, waiting for transfers between devices, per_device(): lax.all_to_all(partial_value, ('expert', 'tensor'), split_axis=0, concat_...  13.2 us
    dot_general x1, matrix products, per_device(): jnp.einsum('lrd,lfd->lrf', rows_in, up_proj, preferred_element_type=jnp.f...  9.69 us
    dot_general x1, matrix products, per_device(): jnp.einsum('lrd,lfd->lrf', rows_in, gate_proj, preferred_element_type=jnp...  9.68 us
    dot_general x1, matrix products, per_device(): jnp.einsum('lrf,lfd->lrd', hidden, down_proj, preferred_element_type=jnp....  7.26 us
    all_to_all x2, other arithmetic, per_device(): lax.all_to_all(copies, ('expert', 'tensor'), split_axis=0, concat_axis=0,...  6.41 us
    all_to_all x1, starting transfers between devices, per_device(): lax.all_to_all(partial_value, ('expert', 'tensor'), split_axis=0, concat_...  5.81 us
  transfers between devices with their start and end apart: 2, of which 2 were waited for; matrix products, arithmetic and copies ran while one was open for 0% of the time, Pallas kernels for 0%

commit v1 on v0

--- a/solution.py
+++ b/solution.py
@@ -36,7 +36,7 @@
     up_part = jnp.einsum("lrd,lfd->lrf", rows_in, up_proj, preferred_element_type=jnp.float32)
     gate_full, up_full = (
         lax.psum(gate_part.astype(jnp.bfloat16), "sub").astype(jnp.float32),
-        lax.psum(up_part.astype(jnp.bfloat16), "sub").astype(jnp.float32),
+        jnp.sum(lax.all_gather(up_part.astype(jnp.bfloat16), "sub"), axis=0).astype(jnp.float32),
     )
     hidden = (jax.nn.silu(gate_full) * up_full).astype(jnp.bfloat16)
     partial_value = jnp.einsum(

time: 120 us -> 110 us (0.917)
  waiting for transfers between devices: 30.3 us -> 18.8 us
  blocking collectives: 20.3 us -> 22.5 us
    psum x1, waiting for transfers between devices: 17.1 us -> 5.54 us  [per_device(): lax.psum(gate_part.astype(jnp.bfloat16), 'sub').astype(jnp.float32)]
    all_gather x0 -> x1, blocking collectives: none -> 2.2 us  [per_device(): lax.all_gather(up_part.astype(jnp.bfloat16), 'sub')]
  transfers between devices with their start and end apart: 2 -> 2, of which waited for: 2 -> 2; matrix products, arithmetic and copies ran while one was open for 0% -> 9% of each run, Pallas kernels for 0% -> 0%
where the time goes in v1:
time: 110 us
  matrix products  27.2 us (25%)
  blocking collectives  22.5 us (20%)
  waiting for transfers between devices  18.8 us (17%)
  other arithmetic  15 us (14%)
  between operations  13.6 us (12%)
  local copies, waits for them, and re-layouts  6.85 us (6%)
  starting transfers between devices  5.82 us (5%)
    all_to_all x1, blocking collectives, per_device(): lax.all_to_all(copies, ('expert', 'tensor'), split_axis=0, concat_axis=0,...  20.3 us
    all_to_all x1, waiting for transfers between devices, per_device(): lax.all_to_all(partial_value, ('expert', 'tensor'), split_axis=0, concat_...  13.2 us
    dot_general x1, matrix products, per_device(): jnp.einsum('lrd,lfd->lrf', rows_in, gate_proj, preferred_element_type=jnp...  9.69 us
    dot_general x1, matrix products, per_device(): jnp.einsum('lrd,lfd->lrf', rows_in, up_proj, preferred_element_type=jnp.f...  9.07 us
    dot_general x1, matrix products, per_device(): jnp.einsum('lrf,lfd->lrd', hidden, down_proj, preferred_element_type=jnp....  7.22 us
    all_to_all x2, other arithmetic, per_device(): lax.all_to_all(copies, ('expert', 'tensor'), split_axis=0, concat_axis=0,...  6.41 us
    all_to_all x1, starting transfers between devices, per_device(): lax.all_to_all(partial_value, ('expert', 'tensor'), split_axis=0, concat_...  5.81 us
    psum x1, waiting for transfers between devices, per_device(): lax.psum(gate_part.astype(jnp.bfloat16), 'sub').astype(jnp.float32)  5.54 us
  transfers between devices with their start and end apart: 2, of which 2 were waited for; matrix products, arithmetic and copies ran while one was open for 9% of the time, Pallas kernels for 0%

profile of v1, /device:TPU:0, one launch (start us, length us, event | category | flops | bytes accessed | tf_op | source)
XLA Modules:
  0.0 109.7 jit_solution(14223483174865200396)
XLA Ops:
  6.5 0.0 copy-start
  6.5 0.0 all-reduce.2.cloned.1.call-start
  6.5 0.8 convert_reduce_fusion.1
  7.4 0.1 and.21
  7.4 0.1 and.23
  7.6 0.1 eq.66
  7.6 0.1 eq.61
  7.7 0.1 eq.64
  7.8 0.0 copy-done
  7.8 0.3 convolution_convert_fusion.1
  8.1 0.2 broadcast_in_dim.4
  8.3 0.2 broadcast_in_dim.5
  8.5 0.5 all_to_all.16
  9.0 0.5 broadcast.69
  9.5 3.5 %reduce.4 = bf16[8,28672]{1,0:T(8,128)(2,1)S(1)} reduce(bf16[8,1,28672]{2,1,0:T(2,128)(2,1)S(1)} %all_to_all.16, bf16[]{:T(256)} %broadcast.69), dimensions={1}, to_apply=%all_to_all.16.reduce_sub_computation | reduce | bytes 917506 | tf_op jit(solution)/shard_map/all_to_all | solution.py:32
  13.0 0.3 reshape.95
  13.4 20.3 %all_to_all.20 = bf16[8,2,14336]{2,1,0:T(2,128)(2,1)S(1)} all-to-all(bf16[8,2,14336]{2,1,0:T(2,128)(2,1)S(1)} %reshape.95), channel_id=1, replica_groups=mesh['groups'=2,'expert'=4,'tensor'=2,'sub'=2] {'expert','tensor'}, dimensions={0} | all-to-all | bytes 917504 | tf_op jit(solution)/shard_map/all_to_all | solution.py:32
  33.7 0.5 reshape.96
  34.1 2.9 %reduce.1 = bf16[8,28672]{1,0:T(8,128)(2,1)S(1)} reduce(bf16[8,1,28672]{2,1,0:T(2,128)(2,1)S(1)} %reshape.96, bf16[]{:T(256)} %constant.19), dimensions={1}, to_apply=%all_to_all.13.reduce_sub_computation | reduce | bytes 917506 | tf_op jit(solution)/shard_map/all_to_all | solution.py:32
  37.0 0.3 reshape.87
  37.3 0.3 copy.17
  37.7 0.2 reshape.88
  37.9 9.7 %convolution_convert_fusion.4 = bf16[4,16,512]{2,1,0:T(8,128)(2,1)} fusion(bf16[4,16,3584]{2,1,0:T(8,128)(2,1)S(1)} %reshape.88, bf16[4,512,3584]{2,1,0:T(8,128)(2,1)} %param.9), kind=kOutput, calls=%fused_computation.4 | convolution fusion | flops 234913792 | bytes 15204352 | tf_op jit(solution)/shard_map/lrd,lfd->lrf/dot_general | solution.py:35
  47.5 0.0 all-reduce.2.cloned.1.call-update
  47.6 9.1 %convolution_convert_fusion.3 = bf16[4,16,512]{2,1,0:T(8,128)(2,1)S(1)} fusion(bf16[4,16,3584]{2,1,0:T(8,128)(2,1)S(1)} %reshape.88, bf16[4,512,3584]{2,1,0:T(8,128)(2,1)} %param.10), kind=kOutput, calls=%fused_computation.3 | convolution fusion | flops 234913792 | bytes 15204352 | tf_op jit(solution)/shard_map/lrd,lfd->lrf/dot_general | solution.py:36
  56.6 0.0 copy-start.1
  56.6 0.0 copy-start.2
  56.6 2.2 %all-gather = bf16[8,16,512]{2,1,0:T(8,128)(2,1)S(1)} all-gather(bf16[4,16,512]{2,1,0:T(8,128)(2,1)S(1)} %convolution_convert_fusion.3), channel_id=2, replica_groups=mesh['groups'=2,'expert'=4,'tensor'=2,'sub'=2] {'sub'}, dimensions={0}, use_global_device_ids=true | all-gather | bytes 196608 | tf_op jit(solution)/shard_map/all_gather | solution.py:39
  58.9 5.5 %all-reduce.2.cloned.1.call-done = bf16[4,16,512]{2,1,0:T(8,128)(2,1)} async-done(((bf16[4,16,512]{2,1,0:T(8,128)(2,1)}), bf16[4,16,512]{2,1,0:T(8,128)(2,1)}) %all-reduce.2.cloned.1.call-update) | async-done | bytes 65552 | tf_op jit(solution)/shard_map/psum | solution.py:38
  64.4 7.2 %convolution_convert_fusion = bf16[4,16,3584]{2,1,0:T(8,128)(2,1)S(1)} fusion(bf16[4,512,3584]{2,1,0:T(8,128)(2,1)} %param.11, bf16[4,16,512]{2,1,0:T(8,128)(2,1)S(1)} %reduce_sum.41, bf16[4,16,512]{2,1,0:T(8,128)(2,1)} %all-reduce.2.cloned.1.call-done), kind=kOutput, calls=%fused_computation | convolution fusion | flops 235372544 | bytes 15269888 | tf_op jit(solution)/shard_map/lrf,lfd->lrd/dot_general | solution.py:42
  71.6 0.2 reshape.89
  71.8 0.3 copy.22
  72.2 0.4 all_to_all.17
  72.5 3.5 %reduce.5 = bf16[8,28672]{1,0:T(8,128)(2,1)S(1)} reduce(bf16[8,1,28672]{2,1,0:T(2,128)(2,1)S(1)} %all_to_all.17, bf16[]{:T(256)} %broadcast.69), dimensions={1}, to_apply=%all_to_all.17.reduce_sub_computation | reduce | bytes 917506 | tf_op jit(solution)/shard_map/all_to_all | solution.py:48
  76.1 1.1 %reshape.97 = bf16[8,2,14336]{2,1,0:T(2,128)(2,1)} reshape(bf16[8,28672]{1,0:T(8,128)(2,1)S(1)} %reduce.5) | data formatting | bytes 917504
  77.2 5.8 %all-to-all-start.1 = ((bf16[8,2,14336]{2,1,0:T(2,128)(2,1)}), bf16[8,2,14336]{2,1,0:T(2,128)(2,1)S(1)}, u32[]{:S(2)}, u32[]{:S(2)}) async-start(bf16[8,2,14336]{2,1,0:T(2,128)(2,1)} %reshape.97), calls=%async_computation.1 | async-start | bytes 917504 | tf_op jit(solution)/shard_map/all_to_all | solution.py:48
  83.0 0.0 copy-done.1
  83.0 0.0 copy-done.2
  83.0 0.1 select_reduce_fusion
  83.1 0.1 fusion.8
  83.2 0.1 mul.29
  83.3 13.2 %all-to-all-done.1 = bf16[8,2,14336]{2,1,0:T(2,128)(2,1)S(1)} async-done(((bf16[8,2,14336]{2,1,0:T(2,128)(2,1)}), bf16[8,2,14336]{2,1,0:T(2,128)(2,1)S(1)}, u32[]{:S(2)}, u32[]{:S(2)}) %all-to-all-start.1) | async-done | bytes 458784 | tf_op jit(solution)/shard_map/all_to_all | solution.py:48
  96.5 0.5 reshape.98
  97.0 2.7 %convert_reduce_fusion = f32[8,28672]{1,0:T(8,128)S(1)} fusion(bf16[8,1,28672]{2,1,0:T(2,128)(2,1)S(1)} %reshape.98), kind=kLoop, calls=%fused_computation.5 | loop fusion | flops 229376 | bytes 1376256 | tf_op jit(solution)/shard_map/convert_element_type | solution.py:52
  99.7 0.5 reshape.91
  100.2 1.3 %reduce_sum.42 = f32[4,28672]{1,0:T(4,128)S(1)} reduce(f32[4,2,28672]{2,1,0:T(2,128)S(1)} %reshape.91, f32[]{:T(128)} %constant.13.clone.1), dimensions={1}, to_apply=%region_5.6 | reduce | flops 114688 | bytes 1376260 | tf_op jit(solution)/shard_map/reduce_sum | solution.py:52
  101.5 0.3 reshape.90
  101.9 0.9 convolution_convert_fusion.2
  (5 shorter events, 0.1 us)
Async XLA Ops:
  6.5 1.3 %copy-start = (bf16[3,3584]{1,0:T(4,128)(2,1)S(1)}, bf16[3,3584]{1,0:T(4,128)(2,1)}, u32[]{:S(2)}) copy-start(bf16[3,3584]{1,0:T(4,128)(2,1)} %param.6) | copy-start | bytes 64516
  6.5 57.9 %all-reduce.2.cloned.1.call-start = ((), (), s32[]{:S(2)}) async-start(), calls=%async_computation.2 | async-start | bytes 131072 | tf_op jit(solution)/shard_map/psum | solution.py:38
  56.6 26.4 %copy-start.1 = (s32[3,8]{1,0:T(4,128)S(1)}, s32[3,8]{1,0:T(4,128)}, u32[]{:S(2)}) copy-start(s32[3,8]{1,0:T(4,128)} %param.7) | copy-start | bytes 292
  56.6 26.4 %copy-start.2 = (f32[3,8]{1,0:T(4,128)S(1)}, f32[3,8]{1,0:T(4,128)}, u32[]{:S(2)}) copy-start(f32[3,8]{1,0:T(4,128)} %param.8) | copy-start | bytes 292
  77.2 19.3 %all-to-all-start.1 = ((bf16[8,2,14336]{2,1,0:T(2,128)(2,1)}), bf16[8,2,14336]{2,1,0:T(2,128)(2,1)S(1)}, u32[]{:S(2)}, u32[]{:S(2)}) async-start(bf16[8,2,14336]{2,1,0:T(2,128)(2,1)} %reshape.97), calls=%async_computation.1 | async-start | bytes 917504 | tf_op jit(solution)/shard_map/all_to_all | solution.py:48
Sparse Core Ops, SparseCore 0:
  47.7 16.6 all-reduce.1
